TPU v7x, 32 devices: a whole 2x2x4 slice. The times are simulated.
32 devices in a mesh: groups: 2 (over x), ctx: 16 (over z, y, core).
Axes of the slice: x: 2, y: 2, z: 4, core: 2. Of those that a mesh axis runs over, the one named last changes fastest.
Arguments:
- queries: bfloat16 [256, 2048], P(('groups', 'ctx')), parts along dimension 0, may hold values from -200 to 200
- slab_keys: bfloat16 [256, 2048], P(('groups', 'ctx')), parts along dimension 0, may hold values from -6 to 6
- slab_values: bfloat16 [256, 2048], P(('groups', 'ctx')), parts along dimension 0, may hold values from -6 to 6
- cache_keys: bfloat16 [16384, 2048], P(('groups', 'ctx')), parts along dimension 0, may hold values from -12 to 12
- cache_values: bfloat16 [16384, 2048], P(('groups', 'ctx')), parts along dimension 0, may hold values from -6 to 6
- offset: int32 [2], P('groups'), parts along dimension 0, may hold values from 2048 to 8192
- slab_len: int32 [2], P('groups'), parts along dimension 0, may hold values from 64 to 128
Outputs:
- attended: bfloat16 [256, 2048], P(('groups', 'ctx')), parts along dimension 0
There are 2 independent parts, one for each index of `groups`. A program takes and returns all parts, laid end to end along the dimension named above; each array names one. Nothing has to cross between parts.
All inputs are finite; a program needn't handle non-finite values.
Results may differ from a plain program's by a relative error of at most 0.0081.
Values may be sent and summed in bfloat16 or wider, within the bound.
A program may use at most 128 MiB of HBM per device.

v0:
```python
import jax
import jax.numpy as jnp
from jax import lax
from jax.sharding import PartitionSpec as P

DH = 128
KB = 256
very_low = -1e30


def block_state(query_heads, key_blocks, value_blocks, visible, score_scale):
    scores = (
        jnp.einsum("qhd,gkhd->qghk", query_heads, key_blocks, preferred_element_type=jnp.float32)
        * score_scale
    )
    visible_head = visible[:, :, None, :]
    masked = jnp.where(visible_head, scores, very_low)
    maxima = jnp.max(masked, axis=3)
    weights = jnp.exp(jnp.where(visible_head, scores - maxima[..., None], -jnp.inf))
    totals = jnp.sum(weights, axis=3)
    rounded = weights.astype(jnp.bfloat16)
    products = jnp.einsum(
        "qghk,gkhd->qghd", rounded, value_blocks, preferred_element_type=jnp.float32
    )
    return (maxima, totals, products)


def absorb(running, terms):
    largest, weight_sum, weighted = running
    maxima, totals, products = terms
    new_largest = jnp.maximum(largest, jnp.max(maxima, axis=1))
    old_factor = jnp.exp(largest - new_largest)
    factors = jnp.exp(maxima - new_largest[:, None, :])
    weight_sum = weight_sum * old_factor + jnp.sum(factors * totals, axis=1)
    weighted = weighted * old_factor[..., None] + jnp.sum(factors[..., None] * products, axis=1)
    return (new_largest, weight_sum, weighted)


def body(queries, slab_keys, slab_values, cache_keys, cache_values, offset, slab_len):
    device_rank = lax.axis_index("ctx")
    device_count = lax.axis_size("ctx")
    own_rows = queries.shape[0]
    slab_rows = own_rows * device_count
    cache_rows = cache_keys.shape[0]
    head_count = queries.shape[1] // DH
    score_scale = DH ** (-0.5)
    gathered = lax.all_gather(queries, "ctx", axis=0, tiled=True)
    query_heads = gathered.reshape(slab_rows, head_count, DH)
    running = (
        jnp.full((slab_rows, head_count), very_low, jnp.float32),
        jnp.zeros((slab_rows, head_count), jnp.float32),
        jnp.zeros((slab_rows, head_count, DH), jnp.float32),
    )
    for block_number in range(cache_rows // KB):
        block_start = block_number * KB
        key_blocks = cache_keys[block_start : block_start + KB].reshape(1, KB, head_count, DH)
        value_blocks = cache_values[block_start : block_start + KB].reshape(1, KB, head_count, DH)
        positions = device_rank * cache_rows + block_start + jnp.arange(KB, dtype=jnp.int32)
        visible = jnp.broadcast_to((positions < offset[0])[None, None, :], (slab_rows, 1, KB))
        running = absorb(
            running, block_state(query_heads, key_blocks, value_blocks, visible, score_scale)
        )
    own_index = device_rank * own_rows + jnp.arange(own_rows, dtype=jnp.int32)
    largest, weight_sum, weighted = running
    quotient = (weighted / jnp.maximum(weight_sum, 1.0)[..., None]).astype(jnp.bfloat16)
    parts_quotient = lax.all_to_all(
        quotient.reshape(1, slab_rows, head_count * DH),
        "ctx",
        split_axis=1,
        concat_axis=0,
        tiled=True,
    )
    parts_sum, parts_largest = (
        lax.all_to_all(weight_sum[None], "ctx", split_axis=1, concat_axis=0, tiled=True),
        lax.all_to_all(largest[None], "ctx", split_axis=1, concat_axis=0, tiled=True),
    )
    own_largest = jnp.max(parts_largest, axis=0)
    factors = jnp.exp(parts_largest - own_largest[None]) * parts_sum
    own_sum = jnp.sum(factors, axis=0)
    own_weighted = jnp.sum(
        factors[..., None]
        * parts_quotient.reshape(device_count, own_rows, head_count, DH).astype(jnp.float32),
        axis=0,
    )
    own_state = (own_largest, own_sum, own_weighted)
    own_queries = queries.reshape(own_rows, head_count, DH)
    keys_piece = lax.all_gather(slab_keys, "ctx", axis=0, tiled=True)
    values_piece = lax.all_gather(slab_values, "ctx", axis=0, tiled=True)
    piece_rows = keys_piece.shape[0]
    piece_blocks = piece_rows // own_rows
    key_index = jnp.arange(piece_rows, dtype=jnp.int32).reshape(piece_blocks, own_rows)
    visible = (key_index[None] <= own_index[:, None, None]) & (key_index[None] < slab_len[0])
    own_state = absorb(
        own_state,
        block_state(
            own_queries,
            keys_piece.reshape(piece_blocks, own_rows, head_count, DH),
            values_piece.reshape(piece_blocks, own_rows, head_count, DH),
            visible,
            score_scale,
        ),
    )
    final_largest, final_sum, final_weighted = own_state
    combined = (final_weighted / final_sum[..., None]).reshape(own_rows, head_count * DH)
    combined = jnp.where((own_index < slab_len[0])[:, None], combined, 0.0)
    return combined.astype(jnp.bfloat16)


def solution(mesh):
    placed = (
        P(("groups", "ctx"), None),
        P(("groups", "ctx"), None),
        P(("groups", "ctx"), None),
        P(("groups", "ctx"), None),
        P(("groups", "ctx"), None),
        P("groups"),
        P("groups"),
    )
    return jax.shard_map(
        body, mesh=mesh, in_specs=placed, out_specs=P(("groups", "ctx"), None), check_vma=False
    )
```

profile of v0, /device:TPU:0, one launch (start us, length us, event | category | flops | bytes accessed | tf_op | source)
XLA Modules:
  0.0 140.0 jit_solution(13504468689925622335)
XLA Ops:
  0.7 1.7 %fusion.59 = (bf16[256,2048]{1,0:T(8,128)(2,1)S(1)}, bf16[256,2048]{1,0:T(8,128)(2,1)S(1)}) fusion(bf16[512,2048]{1,0:T(8,128)(2,1)} %param.10), kind=kLoop, calls=%fused_computation.94 | loop fusion | bytes 4194304 | tf_op jit(solution)/shard_map/slice | solution.py:56
  3.1 24.6 %all_gather.9 = bf16[128,2048]{1,0:T(8,128)(2,1)S(1)} all-gather(bf16[8,2048]{1,0:T(8,128)(2,1)S(1)} %copy-done.5), channel_id=1, replica_groups=mesh['groups'=2,'ctx'=16] {'ctx'}, dimensions={0}, use_global_device_ids=true | all-gather | bytes 557056 | tf_op jit(solution)/shard_map/all_gather | solution.py:47
  28.0 1.3 copy.96
  29.3 0.6 fusion.3
  30.5 0.6 fusion
  32.3 0.7 reduce.7
  33.0 0.7 reshape.418
  33.7 3.5 %all-to-all-start = ((f32[16,1,128]{2,1,0:T(1,128)}), f32[16,1,128]{2,1,0:T(1,128)S(1)}, u32[]{:S(2)}, u32[]{:S(2)}) async-start(f32[16,1,128]{2,1,0:T(1,128)} %reshape.418), calls=%async_computation | async-start | bytes 16384 | tf_op jit(solution)/shard_map/all_to_all | solution.py:75
  37.9 23.2 %all_gather.10 = bf16[128,2048]{1,0:T(8,128)(2,1)S(1)} all-gather(bf16[8,2048]{1,0:T(8,128)(2,1)S(1)} %copy-done.4), channel_id=1, replica_groups=mesh['groups'=2,'ctx'=16] {'ctx'}, dimensions={0}, use_global_device_ids=true | all-gather | bytes 557056 | tf_op jit(solution)/shard_map/all_gather | solution.py:87
  61.2 0.9 copy.112
  62.1 3.1 %fusion.58 = (bf16[256,2048]{1,0:T(8,128)(2,1)}, bf16[256,2048]{1,0:T(8,128)(2,1)}) fusion(bf16[512,2048]{1,0:T(8,128)(2,1)} %param.11), kind=kLoop, calls=%fused_computation.93 | loop fusion | bytes 4194304 | tf_op jit(solution)/shard_map/slice | solution.py:57
  65.1 1.5 %copy.71 = bf16[256,2048]{0,1:T(8,128)(2,1)S(1)} copy(bf16[256,2048]{1,0:T(8,128)(2,1)} %get-tuple-element.16) | data formatting | bytes 2097152 | tf_op jit(solution)/shard_map/slice | solution.py:57
  66.6 3.3 %fusion.12 = f32[128,1,16,128]{0,3,2,1:T(8,128)} fusion(bf16[256,16,128]{0,2,1:T(8,128)(2,1)S(1)} %bitcast.143, f32[16,256,128]{2,1,0:T(8,128)} %copy-done, f32[128,16]{0,1:T(8,128)S(1)} %get-tuple-element.29, pred[256]{0:T(512)(128)(4,1)S(1)} %get-tuple-element.32, f32[128,16]{0,1:T(8,128)S(1)} %get-tuple-element.23), kind=kOutput, calls=%fused_computation.20 | convolution fusion | flops 136577024 | bytes 4210944 | tf_op jit(solution)/shard_map/qghk,gkhd->qghd/dot_general | solution.py:22
  69.9 3.6 %copy.73 = f32[1,128,2048]{2,0,1:T(1,128)} copy(f32[1,128,2048]{1,2,0:T(8,128)} %bitcast.144) | data formatting | bytes 2097152 | tf_op jit(solution)/shard_map/reduce_sum | solution.py:35
  73.6 1.5 %copy.75 = bf16[256,2048]{0,1:T(8,128)(2,1)S(1)} copy(bf16[256,2048]{1,0:T(8,128)(2,1)} %get-tuple-element.17) | data formatting | bytes 2097152 | tf_op jit(solution)/shard_map/slice | solution.py:57
  75.0 1.8 %fusion.13 = f32[128,1,16,128]{0,3,2,1:T(8,128)} fusion(bf16[256,16,128]{0,2,1:T(8,128)(2,1)S(1)} %bitcast.145, f32[16,256,128]{2,1,0:T(8,128)S(1)} %get-tuple-element.28, f32[128,16]{0,1:T(8,128)S(1)} %get-tuple-element.27, pred[256]{0:T(512)(128)(4,1)S(1)} %get-tuple-element.31, f32[128,16]{0,1:T(8,128)S(1)} %get-tuple-element.15), kind=kOutput, calls=%fused_computation.21 | convolution fusion | flops 136577024 | bytes 4210944 | tf_op jit(solution)/shard_map/qghk,gkhd->qghd/dot_general | solution.py:22
  76.8 2.5 %copy.77 = f32[1,128,2048]{2,0,1:T(1,128)S(1)} copy(f32[1,128,2048]{1,2,0:T(8,128)} %bitcast.146) | data formatting | bytes 2097152 | tf_op jit(solution)/shard_map/reduce_sum | solution.py:35
  81.5 3.3 %fusion.60 = bf16[128,1,2048]{2,1,0:T(2,128)(2,1)S(1)} fusion(f32[1,128,2048]{2,0,1:T(1,128)S(1)} %bitcast.152, f32[1,128,2048]{2,0,1:T(1,128)S(1)} %copy.77, f32[1,128,2048]{2,0,1:T(1,128)S(1)} %bitcast.151, f32[1,128,2048]{2,0,1:T(1,128)S(1)} %bitcast.150, f32[1,128,2048]{2,0,1:T(1,128)S(1)} %copy-done.1), kind=kLoop, calls=%fused_computation.96 | loop fusion | flops 1310720 | bytes 5767168
  84.8 0.6 fusion.28
  85.5 0.7 reduce.10
  86.2 0.7 reshape.422
  86.9 3.5 %all-to-all-start.1 = ((f32[16,1,128]{2,1,0:T(1,128)}), f32[16,1,128]{2,1,0:T(1,128)S(1)}, u32[]{:S(2)}, u32[]{:S(2)}) async-start(f32[16,1,128]{2,1,0:T(1,128)} %reshape.422), calls=%async_computation.1 | async-start | bytes 16384 | tf_op jit(solution)/shard_map/all_to_all | solution.py:74
  90.4 23.4 %all_gather.11 = bf16[128,2048]{1,0:T(8,128)(2,1)S(1)} all-gather(bf16[8,2048]{1,0:T(8,128)(2,1)S(1)} %copy-done.6), channel_id=1, replica_groups=mesh['groups'=2,'ctx'=16] {'ctx'}, dimensions={0}, use_global_device_ids=true | all-gather | bytes 557056 | tf_op jit(solution)/shard_map/all_gather | solution.py:88
  114.4 3.7 %reduce.9 = bf16[128,2048]{1,0:T(8,128)(2,1)S(1)} reduce(bf16[128,1,2048]{2,1,0:T(2,128)(2,1)S(1)} %fusion.60, bf16[]{:T(256)} %broadcast.196), dimensions={1}, to_apply=%fusion.60.reduce_sub_computation | reduce | bytes 1048578
  118.1 1.3 reshape.420
  119.4 3.6 %all-to-all-start.2 = ((bf16[16,2,8192]{2,1,0:T(2,128)(2,1)}), bf16[16,2,8192]{2,1,0:T(2,128)(2,1)S(1)}, u32[]{:S(2)}, u32[]{:S(2)}) async-start(bf16[16,2,8192]{2,1,0:T(2,128)(2,1)} %reshape.420), calls=%async_computation.2 | async-start | bytes 1048576 | tf_op jit(solution)/shard_map/all_to_all | solution.py:66
  123.0 0.6 reduce.8
  123.8 0.6 reduce.11
  124.8 0.6 fusion.14
  125.4 11.8 %all-to-all-done.2 = bf16[16,2,8192]{2,1,0:T(2,128)(2,1)S(1)} async-done(((bf16[16,2,8192]{2,1,0:T(2,128)(2,1)}), bf16[16,2,8192]{2,1,0:T(2,128)(2,1)S(1)}, u32[]{:S(2)}, u32[]{:S(2)}) %all-to-all-start.2) | async-done | bytes 524320 | tf_op jit(solution)/shard_map/all_to_all | solution.py:66
  137.8 1.1 bitcast_convert_fusion
  139.3 0.7 fusion.33
  (53 shorter events, 7.3 us)
Async XLA Ops:
  2.3 0.8 copy-start.5
  29.3 1.2 copy-start.2
  29.9 1.4 copy-start
  31.3 6.7 %copy-start.4 = (bf16[8,2048]{1,0:T(8,128)(2,1)S(1)}, bf16[8,2048]{1,0:T(8,128)(2,1)}, u32[]{:S(2)}) copy-start(bf16[8,2048]{1,0:T(8,128)(2,1)} %param.8) | copy-start | bytes 98308
  33.7 53.2 %all-to-all-start = ((f32[16,1,128]{2,1,0:T(1,128)}), f32[16,1,128]{2,1,0:T(1,128)S(1)}, u32[]{:S(2)}, u32[]{:S(2)}) async-start(f32[16,1,128]{2,1,0:T(1,128)} %reshape.418), calls=%async_computation | async-start | bytes 16384 | tf_op jit(solution)/shard_map/all_to_all | solution.py:75
  76.8 2.9 %copy-start.3 = (bf16[16,8,16,128]{3,2,1,0:T(8,128)(2,1)S(1)}, bf16[16,8,16,128]{3,2,1,0:T(8,128)(2,1)}, u32[]{:S(2)}) copy-start(bf16[16,8,16,128]{3,2,1,0:T(8,128)(2,1)} %copy.112) | copy-start | bytes 1572868
  80.3 1.2 copy-start.1
  84.8 5.6 %copy-start.6 = (bf16[8,2048]{1,0:T(8,128)(2,1)S(1)}, bf16[8,2048]{1,0:T(8,128)(2,1)}, u32[]{:S(2)}) copy-start(bf16[8,2048]{1,0:T(8,128)(2,1)} %param.9) | copy-start | bytes 98308
  86.9 32.5 %all-to-all-start.1 = ((f32[16,1,128]{2,1,0:T(1,128)}), f32[16,1,128]{2,1,0:T(1,128)S(1)}, u32[]{:S(2)}, u32[]{:S(2)}) async-start(f32[16,1,128]{2,1,0:T(1,128)} %reshape.422), calls=%async_computation.1 | async-start | bytes 16384 | tf_op jit(solution)/shard_map/all_to_all | solution.py:74
  119.4 17.8 %all-to-all-start.2 = ((bf16[16,2,8192]{2,1,0:T(2,128)(2,1)}), bf16[16,2,8192]{2,1,0:T(2,128)(2,1)S(1)}, u32[]{:S(2)}, u32[]{:S(2)}) async-start(bf16[16,2,8192]{2,1,0:T(2,128)(2,1)} %reshape.420), calls=%async_computation.2 | async-start | bytes 1048576 | tf_op jit(solution)/shard_map/all_to_all | solution.py:66
where the time goes:
time: 141 us; the launch traced here: 140 us
  blocking collectives  71.2 us (50%)
  local copies, waits for them, and re-layouts  23.8 us (17%)
  other arithmetic  13.6 us (10%)
  waiting for transfers between devices  11.9 us (8%)
  starting transfers between devices  10.5 us (7%)
  matrix products  7.41 us (5%)
  between operations  1.62 us (1%)
    all_gather x1, blocking collectives, body(): gathered = lax.all_gather(queries, 'ctx', axis=0, tiled=True)  24.6 us
    all_gather x1, blocking collectives, body(): values_piece = lax.all_gather(slab_values, 'ctx', axis=0, tiled=True)  23.4 us
    all_gather x1, blocking collectives, body(): keys_piece = lax.all_gather(slab_keys, 'ctx', axis=0, tiled=True)  23.2 us
    all_to_all x1, waiting for transfers between devices, body(): lax.all_to_all(quotient.reshape(1, slab_rows, head_count * DH), 'ctx', sp...  11.8 us
    unnamed x5, other arithmetic  8.48 us
    unnamed x25, local copies, waits for them, and re-layouts  7.98 us
    reduce_sum x2, local copies, waits for them, and re-layouts, absorb(): jnp.sum(factors[..., None] * products, axis=1)  6.12 us
    slice x3, local copies, waits for them, and re-layouts, body(): cache_values[block_start:block_start + KB].reshape(1, KB, head_count, DH)  6.04 us
  transfers between devices with their start and end apart: 3, of which 1 were waited for; matrix products, arithmetic and copies ran while one was open for 24% of the time, Pallas kernels for 0%

commit v1 on v0

--- a/solution.py
+++ b/solution.py
@@ -84,7 +84,29 @@
     )
     own_state = (own_largest, own_sum, own_weighted)
     own_queries = queries.reshape(own_rows, head_count, DH)
-    keys_piece = lax.all_gather(slab_keys, "ctx", axis=0, tiled=True)
+    now, top, block_next = (lax.axis_size("ctx"), lax.axis_index("ctx"), slab_keys.shape[0])
+    buffers = []
+    for hop_no in range(now):
+        buffers.append((hop_no, (hop_no + 1) % now))
+    seen = []
+    for hop_no in range(now):
+        seen.append((hop_no, (hop_no - 1) % now))
+    keys_piece = jnp.zeros(
+        (*slab_keys.shape[:0], now * block_next, *slab_keys.shape[1:]), slab_keys.dtype
+    )
+    keys_piece = lax.dynamic_update_slice_in_dim(keys_piece, slab_keys, top * block_next, axis=0)
+    left_arr = val2 = slab_keys
+    step_out = now // 2
+    for num in range(1, step_out + 1):
+        left_arr = lax.ppermute(left_arr, "ctx", buffers)
+        keys_piece = lax.dynamic_update_slice_in_dim(
+            keys_piece, left_arr, (top - num) % now * block_next, axis=0
+        )
+        if num < now - step_out:
+            val2 = lax.ppermute(val2, "ctx", seen)
+            keys_piece = lax.dynamic_update_slice_in_dim(
+                keys_piece, val2, (top + num) % now * block_next, axis=0
+            )
     values_piece = lax.all_gather(slab_values, "ctx", axis=0, tiled=True)
     piece_rows = keys_piece.shape[0]
     piece_blocks = piece_rows // own_rows

time: 141 us -> 161 us (1.14)
  starting transfers between devices: 10.5 us -> 45.1 us
  blocking collectives: 71.2 us -> 45.4 us
  waiting for transfers between devices: 11.9 us -> 22.9 us
    ppermute x0 -> x15, starting transfers between devices: none -> 32.2 us  [the longest x7 31.2 us: body(): val2 = lax.ppermute(val2, 'ctx', seen)]
    all_gather x1 -> x0, blocking collectives: 23.2 us -> none  [body(): keys_piece = lax.all_gather(slab_keys, 'ctx', axis=0, tiled=True)]
    ppermute x0 -> x15, waiting for transfers between devices: none -> 22.9 us  [the longest x8 22.9 us: body(): left_arr = lax.ppermute(left_arr, 'ctx', buffers)]
    all_to_all x1, waiting for transfers between devices: 11.8 us -> 0.01 us  [body(): lax.all_to_all(quotient.reshape(1, slab_rows, head_count * DH), 'ctx', sp...]
    all_gather x1, blocking collectives: 24.6 us -> 20.8 us  [body(): gathered = lax.all_gather(queries, 'ctx', axis=0, tiled=True)]
    all_to_all x1, starting transfers between devices: 3.57 us -> 5.8 us  [body(): lax.all_to_all(quotient.reshape(1, slab_rows, head_count * DH), 'ctx', sp...]
    unnamed x25 -> x29, local copies, waits for them, and re-layouts: 7.98 us -> 7.35 us
  transfers between devices with their start and end apart: 3 -> 18, of which waited for: 1 -> 7; matrix products, arithmetic and copies ran while one was open for 24% -> 26% of each run, Pallas kernels for 0% -> 0%
where the time goes in v1:
time: 161 us
  blocking collectives  45.4 us (28%)
  starting transfers between devices  45.1 us (28%)
  local copies, waits for them, and re-layouts  23.3 us (14%)
  waiting for transfers between devices  22.9 us (14%)
  other arithmetic  14.4 us (9%)
  matrix products  7.41 us (5%)
  between operations  1.98 us (1%)
    ppermute x7, starting transfers between devices, body(): val2 = lax.ppermute(val2, 'ctx', seen)  31.2 us
    all_gather x1, blocking collectives, body(): values_piece = lax.all_gather(slab_values, 'ctx', axis=0, tiled=True)  24.6 us
    ppermute x8, waiting for transfers between devices, body(): left_arr = lax.ppermute(left_arr, 'ctx', buffers)  22.9 us
    all_gather x1, blocking collectives, body(): gathered = lax.all_gather(queries, 'ctx', axis=0, tiled=True)  20.8 us
    unnamed x5, other arithmetic  9.17 us
    unnamed x29, local copies, waits for them, and re-layouts  7.35 us
    reduce_sum x2, local copies, waits for them, and re-layouts, absorb(): jnp.sum(factors[..., None] * products, axis=1)  6.07 us
    slice x3, local copies, waits for them, and re-layouts, body(): cache_values[block_start:block_start + KB].reshape(1, KB, head_count, DH)  6.04 us
  transfers between devices with their start and end apart: 18, of which 7 were waited for; matrix products, arithmetic and copies ran while one was open for 26% of the time, Pallas kernels for 0%

profile of v1, /device:TPU:0, one launch (start us, length us, event | category | flops | bytes accessed | tf_op | source)
XLA Modules:
  0.0 160.5 jit_solution(4372869000990651151)
XLA Ops:
  0.5 5.0 %collective-permute-start.1 = (bf16[8,2048]{1,0:T(8,128)(2,1)}, bf16[8,2048]{1,0:T(8,128)(2,1)S(1)}, u32[]{:S(2)}, u32[]{:S(2)}) collective-permute-start(bf16[8,2048]{1,0:T(8,128)(2,1)} %param.8), channel_id=1, source_target_pairs={{0,15},{1,0},{2,1},{3,2},{4,3},{5,4},{6,5},{7,6},{8,7},{9,8},{10,9... | collective-permute-start | bytes 98312 | tf_op jit(solution)/shard_map/ppermute | solution.py:106
  6.1 1.7 %fusion.59 = (bf16[256,2048]{1,0:T(8,128)(2,1)S(1)}, bf16[256,2048]{1,0:T(8,128)(2,1)S(1)}) fusion(bf16[512,2048]{1,0:T(8,128)(2,1)} %param.10), kind=kLoop, calls=%fused_computation.110 | loop fusion | bytes 4194304 | tf_op jit(solution)/shard_map/slice | solution.py:56
  8.6 20.8 %all_gather.6 = bf16[128,2048]{1,0:T(8,128)(2,1)S(1)} all-gather(bf16[8,2048]{1,0:T(8,128)(2,1)S(1)} %copy-done.7), channel_id=1, replica_groups=mesh['groups'=2,'ctx'=16] {'ctx'}, dimensions={0}, use_global_device_ids=true | all-gather | bytes 557056 | tf_op jit(solution)/shard_map/all_gather | solution.py:47
  29.7 1.3 copy.96
  35.6 3.5 %all-to-all-start = ((f32[16,1,128]{2,1,0:T(1,128)}), f32[16,1,128]{2,1,0:T(1,128)S(1)}, u32[]{:S(2)}, u32[]{:S(2)}) async-start(f32[16,1,128]{2,1,0:T(1,128)} %reshape.418), calls=%async_computation | async-start | bytes 16384 | tf_op jit(solution)/shard_map/all_to_all | solution.py:75
  39.8 3.1 %fusion.58 = (bf16[256,2048]{1,0:T(8,128)(2,1)}, bf16[256,2048]{1,0:T(8,128)(2,1)}) fusion(bf16[512,2048]{1,0:T(8,128)(2,1)} %param.11), kind=kLoop, calls=%fused_computation.109 | loop fusion | bytes 4194304 | tf_op jit(solution)/shard_map/slice | solution.py:57
  42.9 1.5 copy.71
  44.4 3.3 %fusion.12 = f32[128,1,16,128]{0,3,2,1:T(8,128)} fusion(bf16[256,16,128]{0,2,1:T(8,128)(2,1)S(1)} %bitcast.143, f32[16,256,128]{2,1,0:T(8,128)} %copy-done, f32[128,16]{0,1:T(8,128)S(1)} %get-tuple-element.29, pred[256]{0:T(512)(128)(4,1)S(1)} %get-tuple-element.32, f32[128,16]{0,1:T(8,128)S(1)} %get-tuple-element.23), kind=kOutput, calls=%fused_computation.20 | convolution fusion | flops 136577024 | bytes 4210944 | tf_op jit(solution)/shard_map/qghk,gkhd->qghd/dot_general | solution.py:22
  47.7 3.6 %copy.73 = f32[1,128,2048]{2,0,1:T(1,128)} copy(f32[1,128,2048]{1,2,0:T(8,128)} %bitcast.144) | data formatting | bytes 2097152 | tf_op jit(solution)/shard_map/reduce_sum | solution.py:35
  51.3 1.5 copy.75
  52.8 1.8 %fusion.13 = f32[128,1,16,128]{0,3,2,1:T(8,128)} fusion(bf16[256,16,128]{0,2,1:T(8,128)(2,1)S(1)} %bitcast.145, f32[16,256,128]{2,1,0:T(8,128)S(1)} %get-tuple-element.28, f32[128,16]{0,1:T(8,128)S(1)} %get-tuple-element.27, pred[256]{0:T(512)(128)(4,1)S(1)} %get-tuple-element.31, f32[128,16]{0,1:T(8,128)S(1)} %get-tuple-element.15), kind=kOutput, calls=%fused_computation.21 | convolution fusion | flops 136577024 | bytes 4210944 | tf_op jit(solution)/shard_map/qghk,gkhd->qghd/dot_general | solution.py:22
  54.6 2.5 %copy.77 = f32[1,128,2048]{2,0,1:T(1,128)S(1)} copy(f32[1,128,2048]{1,2,0:T(8,128)} %bitcast.146) | data formatting | bytes 2097152 | tf_op jit(solution)/shard_map/reduce_sum | solution.py:35
  57.3 24.6 %all_gather.7 = bf16[128,2048]{1,0:T(8,128)(2,1)} all-gather(bf16[8,2048]{1,0:T(8,128)(2,1)S(1)} %copy-done.6), channel_id=1, replica_groups=mesh['groups'=2,'ctx'=16] {'ctx'}, dimensions={0}, use_global_device_ids=true | all-gather | bytes 557056 | tf_op jit(solution)/shard_map/all_gather | solution.py:110
  83.3 3.8 %fusion.60 = bf16[128,1,2048]{2,1,0:T(2,128)(2,1)S(1)} fusion(f32[1,128,2048]{2,0,1:T(1,128)S(1)} %bitcast.152, f32[1,128,2048]{2,0,1:T(1,128)S(1)} %copy.77, f32[1,128,2048]{2,0,1:T(1,128)S(1)} %bitcast.151, f32[1,128,2048]{2,0,1:T(1,128)S(1)} %bitcast.150, f32[1,128,2048]{2,0,1:T(1,128)S(1)} %copy-done.1), kind=kLoop, calls=%fused_computation.112 | loop fusion | flops 1310720 | bytes 5767168
  88.8 3.7 %all-to-all-start.1 = ((f32[16,1,128]{2,1,0:T(1,128)}), f32[16,1,128]{2,1,0:T(1,128)S(1)}, u32[]{:S(2)}, u32[]{:S(2)}) async-start(f32[16,1,128]{2,1,0:T(1,128)} %reshape.422), calls=%async_computation.1 | async-start | bytes 16384 | tf_op jit(solution)/shard_map/all_to_all | solution.py:74
  93.3 3.7 %reduce.9 = bf16[128,2048]{1,0:T(8,128)(2,1)S(1)} reduce(bf16[128,1,2048]{2,1,0:T(2,128)(2,1)S(1)} %fusion.60, bf16[]{:T(256)} %broadcast.211), dimensions={1}, to_apply=%fusion.60.reduce_sub_computation | reduce | bytes 1048578
  97.0 1.3 reshape.420
  99.1 5.8 %all-to-all-start.2 = ((bf16[16,2,8192]{2,1,0:T(2,128)(2,1)}), bf16[16,2,8192]{2,1,0:T(2,128)(2,1)S(1)}, u32[]{:S(2)}, u32[]{:S(2)}) async-start(bf16[16,2,8192]{2,1,0:T(2,128)(2,1)} %reshape.420), calls=%async_computation.2 | async-start | bytes 1048576 | tf_op jit(solution)/shard_map/all_to_all | solution.py:66
  106.3 4.0 %collective-permute-start.3 = (bf16[8,2048]{1,0:T(8,128)(2,1)S(1)}, bf16[8,2048]{1,0:T(8,128)(2,1)S(1)}, u32[]{:S(2)}, u32[]{:S(2)}) collective-permute-start(bf16[8,2048]{1,0:T(8,128)(2,1)S(1)} %collective-permute-done.1), channel_id=1, source_target_pairs={{0,15},{1,0},{2,1},{3,2},{4,3},{5,4},{6,5},{7,6},{8,7},{9,8},{10,9... | collective-permute-start | bytes 98312 | tf_op jit(solution)/shard_map/ppermute | solution.py:106
  110.3 9.0 %collective-permute-done.2 = bf16[8,2048]{1,0:T(8,128)(2,1)S(1)} collective-permute-done((bf16[8,2048]{1,0:T(8,128)(2,1)S(1)}, bf16[8,2048]{1,0:T(8,128)(2,1)S(1)}, u32[]{:S(2)}, u32[]{:S(2)}) %collective-permute-start.2) | collective-permute-done | bytes 32800 | tf_op jit(solution)/shard_map/ppermute | solution.py:101
  119.3 4.4 %collective-permute-start.5 = (bf16[8,2048]{1,0:T(8,128)(2,1)S(1)}, bf16[8,2048]{1,0:T(8,128)(2,1)S(1)}, u32[]{:S(2)}, u32[]{:S(2)}) collective-permute-start(bf16[8,2048]{1,0:T(8,128)(2,1)S(1)} %collective-permute-done.3), channel_id=1, source_target_pairs={{0,15},{1,0},{2,1},{3,2},{4,3},{5,4},{6,5},{7,6},{8,7},{9,8},{10,9... | collective-permute-start | bytes 98312 | tf_op jit(solution)/shard_map/ppermute | solution.py:106
  123.8 1.6 collective-permute-done.4
  125.4 4.4 %collective-permute-start.7 = (bf16[8,2048]{1,0:T(8,128)(2,1)S(1)}, bf16[8,2048]{1,0:T(8,128)(2,1)S(1)}, u32[]{:S(2)}, u32[]{:S(2)}) collective-permute-start(bf16[8,2048]{1,0:T(8,128)(2,1)S(1)} %collective-permute-done.5), channel_id=1, source_target_pairs={{0,15},{1,0},{2,1},{3,2},{4,3},{5,4},{6,5},{7,6},{8,7},{9,8},{10,9... | collective-permute-start | bytes 98312 | tf_op jit(solution)/shard_map/ppermute | solution.py:106
  129.8 1.6 collective-permute-done.6
  131.4 4.4 %collective-permute-start.9 = (bf16[8,2048]{1,0:T(8,128)(2,1)S(1)}, bf16[8,2048]{1,0:T(8,128)(2,1)S(1)}, u32[]{:S(2)}, u32[]{:S(2)}) collective-permute-start(bf16[8,2048]{1,0:T(8,128)(2,1)S(1)} %collective-permute-done.7), channel_id=1, source_target_pairs={{0,15},{1,0},{2,1},{3,2},{4,3},{5,4},{6,5},{7,6},{8,7},{9,8},{10,9... | collective-permute-start | bytes 98312 | tf_op jit(solution)/shard_map/ppermute | solution.py:106
  135.9 1.6 collective-permute-done.8
  137.5 4.4 %collective-permute-start.11 = (bf16[8,2048]{1,0:T(8,128)(2,1)S(1)}, bf16[8,2048]{1,0:T(8,128)(2,1)S(1)}, u32[]{:S(2)}, u32[]{:S(2)}) collective-permute-start(bf16[8,2048]{1,0:T(8,128)(2,1)S(1)} %collective-permute-done.9), channel_id=1, source_target_pairs={{0,15},{1,0},{2,1},{3,2},{4,3},{5,4},{6,5},{7,6},{8,7},{9,8},{10,9... | collective-permute-start | bytes 98312 | tf_op jit(solution)/shard_map/ppermute | solution.py:106
  141.9 1.6 collective-permute-done.10
  143.5 4.4 %collective-permute-start.13 = (bf16[8,2048]{1,0:T(8,128)(2,1)S(1)}, bf16[8,2048]{1,0:T(8,128)(2,1)S(1)}, u32[]{:S(2)}, u32[]{:S(2)}) collective-permute-start(bf16[8,2048]{1,0:T(8,128)(2,1)S(1)} %collective-permute-done.11), channel_id=1, source_target_pairs={{0,15},{1,0},{2,1},{3,2},{4,3},{5,4},{6,5},{7,6},{8,7},{9,8},{10,9... | collective-permute-start | bytes 98312 | tf_op jit(solution)/shard_map/ppermute | solution.py:106
  148.0 1.6 collective-permute-done.12
  149.6 6.0 %collective-permute-done.14 = bf16[8,2048]{1,0:T(8,128)(2,1)S(1)} collective-permute-done((bf16[8,2048]{1,0:T(8,128)(2,1)S(1)}, bf16[8,2048]{1,0:T(8,128)(2,1)S(1)}, u32[]{:S(2)}, u32[]{:S(2)}) %collective-permute-start.14) | collective-permute-done | bytes 32800 | tf_op jit(solution)/shard_map/ppermute | solution.py:101
  158.3 1.1 bitcast_convert_fusion
  (103 shorter events, 15.9 us)
Async XLA Ops:
  0.0 105.8 %collective-permute-start = (bf16[8,2048]{1,0:T(8,128)(2,1)}, bf16[8,2048]{1,0:T(8,128)(2,1)S(1)}, u32[]{:S(2)}, u32[]{:S(2)}) collective-permute-start(bf16[8,2048]{1,0:T(8,128)(2,1)} %param.8), channel_id=1, source_target_pairs={{0,1},{1,2},{2,3},{3,4},{4,5},{5,6},{6,7},{7,8},{8,9},{9,10},{10,1... | collective-permute-start | bytes 98312 | tf_op jit(solution)/shard_map/ppermute | solution.py:101
  0.5 105.8 %collective-permute-start.1 = (bf16[8,2048]{1,0:T(8,128)(2,1)}, bf16[8,2048]{1,0:T(8,128)(2,1)S(1)}, u32[]{:S(2)}, u32[]{:S(2)}) collective-permute-start(bf16[8,2048]{1,0:T(8,128)(2,1)} %param.8), channel_id=1, source_target_pairs={{0,15},{1,0},{2,1},{3,2},{4,3},{5,4},{6,5},{7,6},{8,7},{9,8},{10,9... | collective-permute-start | bytes 98312 | tf_op jit(solution)/shard_map/ppermute | solution.py:106
  7.9 0.8 copy-start.7
  31.0 1.2 copy-start.2
  31.6 1.4 copy-start
  35.6 53.2 %all-to-all-start = ((f32[16,1,128]{2,1,0:T(1,128)}), f32[16,1,128]{2,1,0:T(1,128)S(1)}, u32[]{:S(2)}, u32[]{:S(2)}) async-start(f32[16,1,128]{2,1,0:T(1,128)} %reshape.418), calls=%async_computation | async-start | bytes 16384 | tf_op jit(solution)/shard_map/all_to_all | solution.py:75
  54.6 2.8 %copy-start.6 = (bf16[8,2048]{1,0:T(8,128)(2,1)S(1)}, bf16[8,2048]{1,0:T(8,128)(2,1)}, u32[]{:S(2)}) copy-start(bf16[8,2048]{1,0:T(8,128)(2,1)} %param.9) | copy-start | bytes 98308
  54.6 27.4 %copy-start.8 = (bf16[8,2048]{1,0:T(8,128)(2,1)S(1)}, bf16[8,2048]{1,0:T(8,128)(2,1)}, u32[]{:S(2)}) copy-start(bf16[8,2048]{1,0:T(8,128)(2,1)} %param.8) | copy-start | bytes 98308
  81.9 1.4 copy-start.1
  82.0 1.0 copy-start.3
  88.8 10.3 %all-to-all-start.1 = ((f32[16,1,128]{2,1,0:T(1,128)}), f32[16,1,128]{2,1,0:T(1,128)S(1)}, u32[]{:S(2)}, u32[]{:S(2)}) async-start(f32[16,1,128]{2,1,0:T(1,128)} %reshape.422), calls=%async_computation.1 | async-start | bytes 16384 | tf_op jit(solution)/shard_map/all_to_all | solution.py:74
  92.7 17.6 %copy-start.4 = (bf16[128,2048]{1,0:T(8,128)(2,1)S(1)}, bf16[128,2048]{1,0:T(8,128)(2,1)}, u32[]{:S(2)}) copy-start(bf16[128,2048]{1,0:T(8,128)(2,1)} %copy-done.3) | copy-start | bytes 1572868
  99.1 58.6 %all-to-all-start.2 = ((bf16[16,2,8192]{2,1,0:T(2,128)(2,1)}), bf16[16,2,8192]{2,1,0:T(2,128)(2,1)S(1)}, u32[]{:S(2)}, u32[]{:S(2)}) async-start(bf16[16,2,8192]{2,1,0:T(2,128)(2,1)} %reshape.420), calls=%async_computation.2 | async-start | bytes 1048576 | tf_op jit(solution)/shard_map/all_to_all | solution.py:66
  105.8 13.5 %collective-permute-start.2 = (bf16[8,2048]{1,0:T(8,128)(2,1)S(1)}, bf16[8,2048]{1,0:T(8,128)(2,1)S(1)}, u32[]{:S(2)}, u32[]{:S(2)}) collective-permute-start(bf16[8,2048]{1,0:T(8,128)(2,1)S(1)} %collective-permute-done), channel_id=1, source_target_pairs={{0,1},{1,2},{2,3},{3,4},{4,5},{5,6},{6,7},{7,8},{8,9},{9,10},{10,1... | collective-permute-start | bytes 98312 | tf_op jit(solution)/shard_map/ppermute | solution.py:101
  106.3 13.1 %collective-permute-start.3 = (bf16[8,2048]{1,0:T(8,128)(2,1)S(1)}, bf16[8,2048]{1,0:T(8,128)(2,1)S(1)}, u32[]{:S(2)}, u32[]{:S(2)}) collective-permute-start(bf16[8,2048]{1,0:T(8,128)(2,1)S(1)} %collective-permute-done.1), channel_id=1, source_target_pairs={{0,15},{1,0},{2,1},{3,2},{4,3},{5,4},{6,5},{7,6},{8,7},{9,8},{10,9... | collective-permute-start | bytes 98312 | tf_op jit(solution)/shard_map/ppermute | solution.py:106
  119.3 6.0 %collective-permute-start.4 = (bf16[8,2048]{1,0:T(8,128)(2,1)S(1)}, bf16[8,2048]{1,0:T(8,128)(2,1)S(1)}, u32[]{:S(2)}, u32[]{:S(2)}) collective-permute-start(bf16[8,2048]{1,0:T(8,128)(2,1)S(1)} %collective-permute-done.2), channel_id=1, source_target_pairs={{0,1},{1,2},{2,3},{3,4},{4,5},{5,6},{6,7},{7,8},{8,9},{9,10},{10,1... | collective-permute-start | bytes 98312 | tf_op jit(solution)/shard_map/ppermute | solution.py:101
  119.3 6.0 %collective-permute-start.5 = (bf16[8,2048]{1,0:T(8,128)(2,1)S(1)}, bf16[8,2048]{1,0:T(8,128)(2,1)S(1)}, u32[]{:S(2)}, u32[]{:S(2)}) collective-permute-start(bf16[8,2048]{1,0:T(8,128)(2,1)S(1)} %collective-permute-done.3), channel_id=1, source_target_pairs={{0,15},{1,0},{2,1},{3,2},{4,3},{5,4},{6,5},{7,6},{8,7},{9,8},{10,9... | collective-permute-start | bytes 98312 | tf_op jit(solution)/shard_map/ppermute | solution.py:106
  125.4 6.0 %collective-permute-start.6 = (bf16[8,2048]{1,0:T(8,128)(2,1)S(1)}, bf16[8,2048]{1,0:T(8,128)(2,1)S(1)}, u32[]{:S(2)}, u32[]{:S(2)}) collective-permute-start(bf16[8,2048]{1,0:T(8,128)(2,1)S(1)} %collective-permute-done.4), channel_id=1, source_target_pairs={{0,1},{1,2},{2,3},{3,4},{4,5},{5,6},{6,7},{7,8},{8,9},{9,10},{10,1... | collective-permute-start | bytes 98312 | tf_op jit(solution)/shard_map/ppermute | solution.py:101
  125.4 6.0 %collective-permute-start.7 = (bf16[8,2048]{1,0:T(8,128)(2,1)S(1)}, bf16[8,2048]{1,0:T(8,128)(2,1)S(1)}, u32[]{:S(2)}, u32[]{:S(2)}) collective-permute-start(bf16[8,2048]{1,0:T(8,128)(2,1)S(1)} %collective-permute-done.5), channel_id=1, source_target_pairs={{0,15},{1,0},{2,1},{3,2},{4,3},{5,4},{6,5},{7,6},{8,7},{9,8},{10,9... | collective-permute-start | bytes 98312 | tf_op jit(solution)/shard_map/ppermute | solution.py:106
  131.4 6.0 %collective-permute-start.8 = (bf16[8,2048]{1,0:T(8,128)(2,1)S(1)}, bf16[8,2048]{1,0:T(8,128)(2,1)S(1)}, u32[]{:S(2)}, u32[]{:S(2)}) collective-permute-start(bf16[8,2048]{1,0:T(8,128)(2,1)S(1)} %collective-permute-done.6), channel_id=1, source_target_pairs={{0,1},{1,2},{2,3},{3,4},{4,5},{5,6},{6,7},{7,8},{8,9},{9,10},{10,1... | collective-permute-start | bytes 98312 | tf_op jit(solution)/shard_map/ppermute | solution.py:101
  131.4 6.0 %collective-permute-start.9 = (bf16[8,2048]{1,0:T(8,128)(2,1)S(1)}, bf16[8,2048]{1,0:T(8,128)(2,1)S(1)}, u32[]{:S(2)}, u32[]{:S(2)}) collective-permute-start(bf16[8,2048]{1,0:T(8,128)(2,1)S(1)} %collective-permute-done.7), channel_id=1, source_target_pairs={{0,15},{1,0},{2,1},{3,2},{4,3},{5,4},{6,5},{7,6},{8,7},{9,8},{10,9... | collective-permute-start | bytes 98312 | tf_op jit(solution)/shard_map/ppermute | solution.py:106
  137.5 6.0 %collective-permute-start.10 = (bf16[8,2048]{1,0:T(8,128)(2,1)S(1)}, bf16[8,2048]{1,0:T(8,128)(2,1)S(1)}, u32[]{:S(2)}, u32[]{:S(2)}) collective-permute-start(bf16[8,2048]{1,0:T(8,128)(2,1)S(1)} %collective-permute-done.8), channel_id=1, source_target_pairs={{0,1},{1,2},{2,3},{3,4},{4,5},{5,6},{6,7},{7,8},{8,9},{9,10},{10,1... | collective-permute-start | bytes 98312 | tf_op jit(solution)/shard_map/ppermute | solution.py:101
  137.5 6.0 %collective-permute-start.11 = (bf16[8,2048]{1,0:T(8,128)(2,1)S(1)}, bf16[8,2048]{1,0:T(8,128)(2,1)S(1)}, u32[]{:S(2)}, u32[]{:S(2)}) collective-permute-start(bf16[8,2048]{1,0:T(8,128)(2,1)S(1)} %collective-permute-done.9), channel_id=1, source_target_pairs={{0,15},{1,0},{2,1},{3,2},{4,3},{5,4},{6,5},{7,6},{8,7},{9,8},{10,9... | collective-permute-start | bytes 98312 | tf_op jit(solution)/shard_map/ppermute | solution.py:106
  143.5 6.0 %collective-permute-start.12 = (bf16[8,2048]{1,0:T(8,128)(2,1)S(1)}, bf16[8,2048]{1,0:T(8,128)(2,1)S(1)}, u32[]{:S(2)}, u32[]{:S(2)}) collective-permute-start(bf16[8,2048]{1,0:T(8,128)(2,1)S(1)} %collective-permute-done.10), channel_id=1, source_target_pairs={{0,1},{1,2},{2,3},{3,4},{4,5},{5,6},{6,7},{7,8},{8,9},{9,10},{10,1... | collective-permute-start | bytes 98312 | tf_op jit(solution)/shard_map/ppermute | solution.py:101
  143.5 6.0 %collective-permute-start.13 = (bf16[8,2048]{1,0:T(8,128)(2,1)S(1)}, bf16[8,2048]{1,0:T(8,128)(2,1)S(1)}, u32[]{:S(2)}, u32[]{:S(2)}) collective-permute-start(bf16[8,2048]{1,0:T(8,128)(2,1)S(1)} %collective-permute-done.11), channel_id=1, source_target_pairs={{0,15},{1,0},{2,1},{3,2},{4,3},{5,4},{6,5},{7,6},{8,7},{9,8},{10,9... | collective-permute-start | bytes 98312 | tf_op jit(solution)/shard_map/ppermute | solution.py:106
  149.5 6.0 %collective-permute-start.14 = (bf16[8,2048]{1,0:T(8,128)(2,1)S(1)}, bf16[8,2048]{1,0:T(8,128)(2,1)S(1)}, u32[]{:S(2)}, u32[]{:S(2)}) collective-permute-start(bf16[8,2048]{1,0:T(8,128)(2,1)S(1)} %collective-permute-done.12), channel_id=1, source_target_pairs={{0,1},{1,2},{2,3},{3,4},{4,5},{5,6},{6,7},{7,8},{8,9},{9,10},{10,1... | collective-permute-start | bytes 98312 | tf_op jit(solution)/shard_map/ppermute | solution.py:101
  155.7 1.5 copy-start.5
